TPU v7x, 32 devices: a whole 2x2x4 slice. The times are simulated.
32 devices in a mesh: rep: 4 (over x, core), shard: 8 (over z, y).
Axes of the slice: x: 2, y: 2, z: 4, core: 2. Of those that a mesh axis runs over, the one named last changes fastest.
Arguments:
- inputs: bfloat16 [32, 1024, 1024], P(('rep', 'shard')), may hold values from -6 to 6
- cotangent: bfloat16 [32, 1024, 1024], P(('rep', 'shard')), may hold values from -6 to 6
- lengths: int32 [32], P(('rep', 'shard')), may hold values from 256 to 1024, as said below
- adapter_ids: int32 [32], P(('rep', 'shard')), may hold values from 0 to 7
- gain_one: float32 [1024], replicated, may hold values from 0.25 to 1.75
- gain_two: float32 [1024], replicated, may hold values from 0.25 to 1.75
- qkv_weight: bfloat16 [1024, 3072], P('shard'), may hold values from -0.1875 to 0.1875
- out_weight: bfloat16 [1024, 1024], P('shard'), may hold values from -0.75 to 0.75
- up_weight: bfloat16 [1024, 4096], P('shard'), may hold values from -0.1875 to 0.1875
- down_weight: bfloat16 [4096, 1024], P('shard'), may hold values from -0.09375 to 0.09375
- adapter_down: bfloat16 [1024, 512], P('shard'), may hold values from -0.1875 to 0.1875
- adapter_up: bfloat16 [1024, 512], P('shard'), may hold values from -1.5 to 1.5
Outputs:
- layer_output: bfloat16 [32, 1024, 1024], P(('rep', 'shard'))
- input_grad: bfloat16 [32, 1024, 1024], P(('rep', 'shard'))
- adapter_down_grad: float32 [1024, 512], P('shard')
- adapter_up_grad: float32 [1024, 512], P('shard')
Inputs may be any that keep to these rules, and one draw needn't show every extreme that they name: `lengths`: every draw has a slot of length 1024.
All inputs are finite; a program needn't handle non-finite values.
Results may differ from a plain program's by a relative error of at most 0.015.
The roundings to bfloat16 on the way count: a program that leaves them out, or rounds other values in their place, can miss the bound.
Values may be sent and summed in bfloat16 or wider, within the bound.
A program may use at most 256 MiB of HBM per device.

v0:
```python
import functools

import jax
import jax.numpy as jnp
from jax import lax
from jax.experimental import pallas as pl
from jax.experimental.pallas import tpu as pltpu
from jax.sharding import PartitionSpec as P

MESH = pl.DeviceIdType.MESH

def mesh_split(n_rep, n_shard):
    zs = 4 if n_shard % 4 == 0 else n_shard
    return zs, n_shard // zs

def share_rows(rows):
    return max(16, rows * 3 // 8 // 16 * 16)


EPS = 1e-05
HEAD = 64
RANK = 16
ADAPTERS = 8
COLS = 4 * RANK
VMEM_CAP = 60 * 1024 * 1024
BF = jnp.bfloat16
F32 = jnp.float32


def dense(left, right):
    return jnp.dot(left, right, preferred_element_type=F32)


def dense_trans(left, right):
    return lax.dot_general(left, right, (((1,), (1,)), ((), ())), preferred_element_type=F32)


def dense_left(left, right):
    return lax.dot_general(left, right, (((0,), (0,)), ((), ())), preferred_element_type=F32)


def lane_group(values, size, group):
    lanes = lax.broadcasted_iota(jnp.int32, values.shape, 1)
    return jnp.where(lanes // size == group, values, jnp.zeros_like(values))


def norm_stats(values):
    center = values - jnp.mean(values, axis=-1, keepdims=True)
    rs = lax.rsqrt(jnp.mean(center * center, axis=-1, keepdims=True) + EPS)
    return center * rs, rs


def norm_back(unit, rs, gain, grad):
    eg = grad * gain
    return rs * (eg - jnp.mean(eg, axis=-1, keepdims=True) - unit * jnp.mean(eg * unit, axis=-1, keepdims=True))


def attn_fwd_body(tile, q_ref, k_ref, v_ref, ctx_ref, p_ref):
    seq, lanes = q_ref.shape
    heads = lanes // HEAD
    scale = HEAD ** (-0.5)
    rows = lax.broadcasted_iota(jnp.int32, (tile, tile), 0)
    cols = lax.broadcasted_iota(jnp.int32, (tile, tile), 1)
    keep = rows >= cols
    off = 0
    for i in range(seq // tile):
        stop = (i + 1) * tile
        q = q_ref[pl.ds(i * tile, tile), :] * jnp.asarray(scale, BF)
        acc = None
        for h in range(heads):
            qh = lane_group(q, HEAD, h)
            s = dense_trans(qh, k_ref[pl.ds(0, stop), :])
            diag = jnp.where(keep, s[:, stop - tile :], -1e30)
            s = diag if i == 0 else jnp.concatenate([s[:, : stop - tile], diag], axis=1)
            peak = jnp.max(s, axis=-1, keepdims=True)
            e = jnp.exp(s - peak)
            inv = 1.0 / jnp.sum(e, axis=-1, keepdims=True)
            p = (e * inv).astype(BF)
            p_ref[h, :, pl.ds(off, stop)] = p
            o = dense(p, lane_group(v_ref[pl.ds(0, stop), :], HEAD, h))
            acc = o if acc is None else acc + o
        ctx_ref[pl.ds(i * tile, tile), :] = acc.astype(BF)
        off += stop


def attn_bwd_body(tile, q_ref, k_ref, v_ref, go_ref, ctx_ref, p_ref, dq_ref, dk_ref, dv_ref, dk_acc, dv_acc):
    seq, lanes = q_ref.shape
    heads = lanes // HEAD
    scale = HEAD ** (-0.5)
    off = 0
    n = seq // tile
    dk_acc[...] = jnp.zeros_like(dk_acc)
    dv_acc[...] = jnp.zeros_like(dv_acc)
    for i in range(n):
        stop = (i + 1) * tile
        sl = pl.ds(i * tile, tile)
        past = pl.ds(0, stop)
        go = go_ref[sl, :]
        q = q_ref[sl, :]
        prod = go.astype(F32) * ctx_ref[sl, :].astype(F32)
        acc = None
        for h in range(heads):
            delta = jnp.sum(lane_group(prod, HEAD, h), axis=-1, keepdims=True)
            gh = lane_group(go, HEAD, h)
            p = p_ref[h, :, pl.ds(off, stop)]
            dp = dense_trans(gh, v_ref[past, :])
            ds = (p.astype(F32) * (dp - delta)).astype(BF)
            dv_acc[past, :] += dense_left(p, gh)
            dk_acc[past, :] += dense_left(ds, lane_group(q, HEAD, h))
            o = dense(ds, lane_group(k_ref[past, :], HEAD, h))
            acc = o if acc is None else acc + o
        dq_ref[sl, :] = (acc * scale).astype(BF)
        off += stop
    dk_ref[...] = (dk_acc[...] * scale).astype(BF)
    dv_ref[...] = dv_acc[...].astype(BF)


def attention_backward(proj, grad_ctx, ctx, probs, tile, lanes=128):
    seq = proj.shape[0]
    width = proj.shape[1] // 3
    n = width // lanes
    heads = lanes // HEAD
    packed = probs.shape[2]
    blk = pl.BlockSpec((seq, lanes), lambda j: (0, j))
    return pl.pallas_call(
        functools.partial(attn_bwd_body, tile),
        grid=(n,),
        out_shape=[jax.ShapeDtypeStruct((seq, width), BF)] * 3,
        in_specs=[pl.BlockSpec((seq, lanes), lambda j, t=t: (0, t * n + j)) for t in range(3)]
        + [blk, blk, pl.BlockSpec((heads, tile, packed), lambda j: (j, 0, 0))],
        out_specs=[blk] * 3,
        scratch_shapes=[pltpu.VMEM((seq, lanes), F32)] * 2,
        compiler_params=pltpu.CompilerParams(vmem_limit_bytes=VMEM_CAP),
        name="attention_backward",
    )(proj, proj, proj, grad_ctx, ctx, probs)


def tail_body(
    x_ref, gh_ref, inner_ref, dq_ref, dk_ref, dv_ref, g_ref, w_ref, adn_ref, aup_ref, din_ref, uin_ref,
    id_ref, gx_ref, pay_ref, dgrad_ref, ugrad_ref,
):
    step = pl.program_id(0)
    dim = x_ref.shape[1]
    thirds = [dq_ref[...], dk_ref[...], dv_ref[...]]
    gi = None
    gn = None
    for p in range(3):
        one = lane_group(dense(thirds[p], aup_ref[...]), RANK, p)
        gi = one if gi is None else gi + one
        g = dense_trans(thirds[p], w_ref[:, pl.ds(p * dim, dim)])
        gn = g if gn is None else gn + g
    gi = gi.astype(BF)
    gn = gn + dense_trans(gi, adn_ref[...])
    unit, rs = norm_stats(x_ref[...].astype(F32))
    normed = (unit * g_ref[...]).astype(BF)
    gx_ref[...] = (gh_ref[...] + norm_back(unit, rs, g_ref[...], gn)).astype(BF)

    @pl.when(step == 0)
    def _():
        dgrad_ref[...] = din_ref[...]
        ugrad_ref[...] = uin_ref[...]

    dgrad_ref[...] += dense_left(gi, normed)
    up = None
    for p in range(3):
        one = dense_left(lane_group(inner_ref[...], RANK, p), thirds[p])
        up = one if up is None else up + one
    ugrad_ref[...] += up

    @pl.when(step == pl.num_programs(0) - 1)
    def _():
        n, pay, width = pay_ref.shape
        mark = jnp.full((pay - 2 * COLS, width), id_ref[0], jnp.int32).astype(F32)
        for i in range(n):
            sl = pl.ds(i * width, width)
            pay_ref[i] = jnp.concatenate([dgrad_ref[:, sl], ugrad_ref[:, sl], mark], axis=0).astype(BF)


def tail_backward(x, gh, inner, dq, dk, dv, gain, qkv, adn, aup, din, uin, adapter, n_shard, rows=256):
    seq, dim = x.shape
    row = pl.BlockSpec((rows, dim), lambda i: (i, 0))

    def whole(shape):
        return pl.BlockSpec(shape, lambda i: (0, 0), pipeline_mode=pl.Buffered(1))

    return pl.pallas_call(
        tail_body,
        grid=(seq // rows,),
        out_shape=[
            jax.ShapeDtypeStruct((seq, dim), BF),
            jax.ShapeDtypeStruct((n_shard, PAY, dim // n_shard), BF),
        ],
        in_specs=[
            row, row, pl.BlockSpec((rows, COLS), lambda i: (i, 0)), row, row, row,
            whole((1, dim)), whole(qkv.shape), whole((dim, COLS)), whole((dim, COLS)), whole((COLS, dim)), whole((COLS, dim)),
            pl.BlockSpec(memory_space=pltpu.SMEM),
        ],
        out_specs=[row, pl.BlockSpec((n_shard, PAY, dim // n_shard), lambda i: (0, 0, 0))],
        scratch_shapes=[pltpu.VMEM((COLS, dim), F32)] * 2,
        compiler_params=pltpu.CompilerParams(vmem_limit_bytes=VMEM_CAP),
        name="tail_backward",
    )(x, gh, inner, dq, dk, dv, gain, qkv, adn, aup, din, uin, adapter)


class Mover:
    def __init__(self, zs, ys, shards, lands, sems, chunks, ahead):
        self.ahead = ahead
        self.zs, self.ys, self.shards, self.lands, self.sems, self.chunks = zs, ys, shards, lands, sems, chunks
        self.r = lax.axis_index("rep")
        self.s = lax.axis_index("shard")
        self.z, self.y = self.s // ys, lax.rem(self.s, ys)
        self.core = lax.rem(self.r, 2)
        self.xp = lax.rem(self.r // 2, 2)
        self.sib = (self.r + 1 - 2 * self.core, self.s)
        self.par = (self.r + 2 - 4 * self.xp, self.s)
        self.ypeers = [lax.rem(self.y + k, ys) for k in range(1, ys)]

    def at_z(self, off):
        return lax.rem(self.z + off, self.zs)

    def barrier(self):
        peers = [(self.r, self.at_z(k) * self.ys + self.y) for k in range(1, self.zs)]
        peers += [(self.r, self.z * self.ys + v) for v in self.ypeers] + [self.par, self.sib]
        bar = pltpu.get_barrier_semaphore()
        for p in peers:
            pl.semaphore_signal(bar, inc=1, device_id=p, device_id_type=MESH)
        pl.semaphore_wait(bar, len(peers))

    def geom(self, t, dest_z):
        w, offs, rows, c0, cols, turn = self.chunks[t]
        a = share_rows(rows)
        half = cols // 2
        mine = pl.ds(pl.multiple_of(self.xp * a, 16), rows - a)
        excl = pl.ds(pl.multiple_of(self.xp * (rows - a), 16), a)
        missing = pl.ds(pl.multiple_of((1 - self.xp) * (rows - a), 16), a)
        first = c0 + self.core * half
        if turn is not None:
            k, span = turn
            first = first + lax.rem(dest_z + k, self.zs) * span
        return w, offs, rows, a, half, mine, excl, missing, pl.ds(pl.multiple_of(first, 128), half)

    def send(self, src, w, zz, yy, rows, col, t, stage, device):
        pltpu.make_async_remote_copy(
            src_ref=src, dst_ref=self.lands[w].at[zz, yy, rows, col], send_sem=self.sems[2 * stage].at[t],
            recv_sem=self.sems[2 * stage + 1].at[t], device_id=device, device_id_type=MESH,
        ).start()

    def relay(self, w, zz, yy, rows, col, t, stage, device):
        self.send(self.lands[w].at[zz, yy, rows, col], w, zz, yy, rows, col, t, stage, device)

    def wait(self, t, stage, side):
        w, offs, rows, a, half, *_ = self.geom(t, self.z)
        far = len([o for o in offs if o])
        near = len(offs) * (self.ys - 1)
        count = ((far * (rows - a)), near * (rows - a), (far + near) * a, (far + near) * rows)[stage]
        if count == 0:
            return
        sem = self.sems[2 * stage + side].at[t]
        elems = count * half
        for out in self.lands:
            _, _, big_r, big_n = out.shape
            for lead in range(1, self.zs + 1):
                for take in range(big_r, 0, -16):
                    if elems % (lead * take * 128) == 0 and elems // (lead * take) <= big_n:
                        reg = out.at[pl.ds(0, lead), 0, pl.ds(0, take), pl.ds(0, elems // (lead * take))]
                        pltpu.make_async_copy(reg, reg, sem).wait()
                        return
        raise ValueError("no region")

    def start_z(self, t):
        offs = self.chunks[t][1]
        for k in range(1, self.zs):
            if (self.zs - k) % self.zs in offs:
                zz = self.at_z(k)
                w, _, _, _, _, mine, _, _, col = self.geom(t, zz)
                self.send(self.shards[w].at[mine, col], w, self.z, self.y, mine, col, t, 0, (self.r, zz * self.ys + self.y))

    def start_y(self, t):
        w, offs, _, _, _, mine, _, _, col = self.geom(t, self.z)
        if 0 in offs:
            for v in self.ypeers:
                self.send(self.shards[w].at[mine, col], w, self.z, self.y, mine, col, t, 1, (self.r, self.z * self.ys + v))

    def begin(self):
        for t in range(min(self.ahead, len(self.chunks))):
            self.start_z(t)
            self.start_y(t)

    def relay_z(self, m):
        if m + self.ahead < len(self.chunks):
            self.start_z(m + self.ahead)
            self.start_y(m + self.ahead)
        w, offs, rows, a, half, mine, excl, missing, col = self.geom(m, self.z)
        self.wait(m, 0, 1)
        for o in offs:
            if o:
                for v in self.ypeers:
                    self.relay(w, self.at_z(o), self.y, mine, col, m, 1, (self.r, self.z * self.ys + v))
        for o in offs:
            if o:
                self.relay(w, self.at_z(o), self.y, excl, col, m, 2, self.par)
                self.relay(w, self.at_z(o), self.y, mine, col, m, 3, self.sib)

    def relay_y(self, m):
        w, offs, rows, a, half, mine, excl, missing, col = self.geom(m, self.z)
        self.wait(m, 1, 1)
        for o in offs:
            for v in self.ypeers:
                self.relay(w, self.at_z(o), v, excl, col, m, 2, self.par)
                self.relay(w, self.at_z(o), v, mine, col, m, 3, self.sib)

    def relay_x(self, m):
        w, offs, rows, a, half, mine, excl, missing, col = self.geom(m, self.z)
        self.wait(m, 2, 1)
        for o in offs:
            if o:
                self.relay(w, self.at_z(o), self.y, missing, col, m, 3, self.sib)
            for v in self.ypeers:
                self.relay(w, self.at_z(o), v, missing, col, m, 3, self.sib)

    def tick(self, todo):
        for stage, m in todo:
            (self.relay_z, self.relay_y, self.relay_x)[stage](m)

    def arrived(self, t):
        self.wait(t, 3, 1)

    def sent(self, t):
        for stage in range(4):
            self.wait(t, stage, 0)


QKV, ADN, AUP, OUT, UP, DOWN = range(6)
AHEAD = 6
UNIT = (4.1, 3.9, 4.0)


class Plan:
    def __init__(self, groups, pairs, zs, n_rb, n, ahead):
        self.pairs = pairs
        self.proj, self.att = [], []
        cost = [5.0, 3.0]
        need = {1: [0, 1]}
        for g in range(groups):
            for k in range(3):
                self.proj.append(len(cost))
                need[len(cost)] = [2 + 3 * g + k]
                cost.append(3.3)
            self.att.append(len(cost))
            cost += [3.45] * pairs
        done = 2 + 3 * groups
        self.out = len(cost)
        need[self.out] = list(range(done, done + groups))
        cost.append(6.0)
        done += groups
        self.ff = len(cost)
        per = (n - done) // zs
        for f in range(zs):
            need[len(cost)] = list(range(done + f * per, done + (f + 1) * per))
            cost += [3.6] * n_rb
        self.end = len(cost)
        cost += [3.6] * n_rb
        self.steps = len(cost)
        self.ticks = {}
        self.spread(cost, need, n, ahead)

    def spread(self, cost, need, n, ahead):
        hop, now = 1.5, 2.0
        free = [now, now, now]
        due = [{}, {}, {}]
        nxt = [0, 0, 0]
        ready = {}

        def begin(c, t):
            free[0] = max(free[0], t) + UNIT[0]
            due[0][c] = free[0] + hop
            free[1] = max(free[1], t) + UNIT[1] / 4

        def run(stage, t):
            c = nxt[stage]
            nxt[stage] += 1
            if stage == 0:
                if c + ahead < n:
                    begin(c + ahead, t)
                free[1] = max(free[1], t) + UNIT[1] * 0.75
                due[1][c] = free[1] + hop
                free[2] = max(free[2], t) + UNIT[2] * 0.43
            elif stage == 1:
                free[2] = max(free[2], t) + UNIT[2] * 0.57
                due[2][c] = free[2] + hop
            else:
                ready[c] = t + 2.0
            return (stage, c)

        def open_ops():
            return [(due[k][nxt[k]], k) for k in range(3) if nxt[k] in due[k]]

        for c in range(min(n, ahead)):
            begin(c, now)
        for step, spent in enumerate(cost):
            todo = []
            if step:
                wanted = need.get(step, [])
                if step == len(cost) - 1:
                    wanted = range(n)
                while True:
                    ops = [v for v in open_ops() if v[0] <= now]
                    if not ops:
                        if all(c in ready for c in wanted):
                            break
                        ops = open_ops()
                    at, stage = min(ops)
                    now = max(now, at)
                    todo.append(run(stage, now))
                for c in wanted:
                    now = max(now, ready[c])
            if todo:
                self.ticks[step] = todo
            now += spent
        self.estimate = now


def layer_body(
    zs, ys, tile, chunks, plan, n_rb, len_ref, id_ref, x_ref, cot_ref, g1_ref, g_ref, qkv_s, adn_s, aup_s, out_s, up_s, down_s,
    qkv_f, proj_ref, inner_ref, adn_ref, aup_ref, ctx_ref, p_ref, y_ref, gh_ref, gc_ref, dgrad_ref, ugrad_ref,
    qa, qb, out_v, up_v, down_v, hid, mlp_acc, gn_acc, nt, io, local, qsem, *sems,
):
    step = pl.program_id(0)
    seq, dim = x_ref.shape
    rows = seq // n_rb
    span = up_v.shape[3] // zs
    mover = Mover(zs, ys, (qkv_s, adn_s, aup_s, out_s, up_s, down_s), (qkv_f, qa, qb, out_v, up_v, down_v), sems, chunks, AHEAD)
    own = [
        pltpu.make_async_copy(src, land.at[mover.z, mover.y], local.at[i])
        for i, (src, land) in enumerate(zip(mover.shards, mover.lands))
    ]

    @pl.when(step == 0)
    def _():
        for cp in own:
            cp.start()
        mover.barrier()
        mover.begin()

        def one(i, carry):
            sl = pl.ds(pl.multiple_of(i * rows, rows), rows)
            unit, _ = norm_stats(x_ref[sl, :].astype(F32))
            nt[sl, :] = (unit * g1_ref[...]).astype(BF)
            return carry

        lax.fori_loop(0, n_rb, one, 0)
        for cp in own:
            cp.wait()

    for at, todo in plan.ticks.items():

        @pl.when(step == at)
        def _():
            mover.tick(todo)

    @pl.when(step == 1)
    def _():
        for t in range(2):
            mover.arrived(t)
        wide = qa.shape[3]
        pick = lax.broadcasted_iota(jnp.int32, (wide, COLS), 0) == lax.broadcasted_iota(jnp.int32, (wide, COLS), 1) + id_ref[0] * COLS
        pick = jnp.where(pick, 1.0, 0.0).astype(BF)
        adn_ref[...] = dense(qa[...].reshape(dim, wide), pick).astype(BF)
        aup_ref[...] = dense(qb[...].reshape(dim, wide), pick).astype(BF)
        inner_ref[...] = dense(nt[...], adn_ref[...]).astype(BF)
        for t in range(2):
            mover.sent(t)

    part = qa.shape[3]
    for i, at in enumerate(plan.proj):
        c0 = (i % 3) * dim + (i // 3) * part
        buf = (qa, qb)[i % 2]

        @pl.when(step == at)
        def _():
            mover.arrived(2 + i)
            cp = pltpu.make_async_copy(qkv_f.at[:, :, :, pl.ds(c0, part)], buf, qsem)
            cp.start()
            cp.wait()

            def one(b, carry):
                sl = pl.ds(pl.multiple_of(b * rows, rows), rows)
                w = buf[...].reshape(dim, part)
                inner = lane_group(inner_ref[sl, :], RANK, i % 3)
                proj_ref[sl, pl.ds(c0, part)] = (
                    dense(nt[sl, :], w) + dense_trans(inner, aup_ref[pl.ds((i // 3) * part, part), :])
                ).astype(BF)
                return carry

            lax.fori_loop(0, n_rb, one, 0)

    lanes = dim // (plan.pairs * len(plan.att))
    for g, base in enumerate(plan.att):

        @pl.when((step >= base) & (step < base + plan.pairs))
        def _():
            first = (step - base + g * plan.pairs) * lanes

            def cut(ref, third):
                return ref.at[:, pl.ds(pl.multiple_of(third * dim + first, 128), lanes)]

            attn_fwd_body(tile, cut(proj_ref, 0), cut(proj_ref, 1), cut(proj_ref, 2), cut(ctx_ref, 0), p_ref)

    def valid_rows(first):
        return first + lax.broadcasted_iota(jnp.int32, (rows, 1), 0) < len_ref[0]

    @pl.when(step == plan.out)
    def _():
        for t in range(len(chunks)):
            if chunks[t][0] == OUT:
                mover.arrived(t)

        def one(i, carry):
            sl = pl.ds(pl.multiple_of(i * rows, rows), rows)
            ctx = ctx_ref[sl, :]
            inner_out = lane_group(dense(ctx, adn_ref[...]), RANK, 3).astype(BF)
            io[sl, :] = inner_out
            hidden = x_ref[sl, :].astype(F32) + (dense(ctx, out_v[...].reshape(dim, dim)) + dense_trans(inner_out, aup_ref[...]))
            hid[sl, :] = hidden
            unit, _ = norm_stats(hidden)
            nt[sl, :] = (unit * g_ref[...]).astype(BF)
            return carry

        lax.fori_loop(0, n_rb, one, 0)

    for k in range(zs):

        @pl.when(step == plan.ff + k * n_rb)
        def _():
            for t in range(len(chunks)):
                if chunks[t][0] == DOWN and chunks[t][1] == (k,) or chunks[t][0] == UP and chunks[t][5][0] == k:
                    mover.arrived(t)

    @pl.when((step >= plan.ff) & (step < plan.end))
    def _():
        at = step - plan.ff
        fz = lax.rem(mover.z + at // n_rb, zs)
        first = lax.rem(at, n_rb) * rows
        sl = pl.ds(pl.multiple_of(first, rows), rows)
        cot = cot_ref[...]
        grad_mlp = jnp.where(valid_rows(first), cot, jnp.zeros_like(cot))
        sub = min(512, span)
        shard_rows = down_v.shape[2]
        k0 = 0.7978845608028654
        for h in range(span // sub):
            up_w = up_v[:, :, :, pl.ds(pl.multiple_of(fz * span + h * sub, 128), sub)].reshape(dim, sub)
            per = sub // shard_rows
            if per:
                down_w = down_v[fz, pl.ds(h * per, per)].reshape(sub, dim)
            else:
                down_w = down_v[fz, h * sub // shard_rows, pl.ds(h * sub % shard_rows, sub)]
            u = dense(nt[sl, :], up_w)
            ga = dense_trans(grad_mlp, down_w)
            sq = u * u
            t = jnp.tanh(k0 * (u + 0.044715 * u * sq))
            half = 0.5 * (1.0 + t)
            act = (u * half).astype(BF)
            d = half + 0.5 * u * (1.0 - t * t) * (k0 * (1.0 + (3.0 * 0.044715) * sq))
            gp = (ga * d).astype(BF)
            m_new = dense(act, down_w)
            g_new = dense_trans(gp, up_w)
            if h == 0:

                @pl.when(at < n_rb)
                def _():
                    mlp_acc[sl, :] = m_new
                    gn_acc[sl, :] = g_new

                @pl.when(at >= n_rb)
                def _():
                    mlp_acc[sl, :] += m_new
                    gn_acc[sl, :] += g_new
            else:
                mlp_acc[sl, :] += m_new
                gn_acc[sl, :] += g_new

    @pl.when(step >= plan.end)
    def _():
        first = (step - plan.end) * rows
        sl = pl.ds(pl.multiple_of(first, rows), rows)
        valid = valid_rows(first)
        hidden = hid[sl, :]
        cot = cot_ref[...]
        y_ref[...] = jnp.where(valid, hidden + mlp_acc[sl, :], 0.0).astype(BF)
        unit, rs = norm_stats(hidden)
        gh = jnp.where(valid, cot, jnp.zeros_like(cot)).astype(F32) + norm_back(unit, rs, g_ref[...], gn_acc[sl, :])
        gh_ref[...] = gh
        ga = gh.astype(BF)
        gio = lane_group(dense(ga, aup_ref[...]), RANK, 3).astype(BF)
        gc_ref[...] = (dense_trans(ga, out_v[...].reshape(dim, dim)) + dense_trans(gio, adn_ref[...])).astype(BF)

        @pl.when(step == plan.end)
        def _():
            dgrad_ref[...] = jnp.zeros_like(dgrad_ref)
            ugrad_ref[...] = jnp.zeros_like(ugrad_ref)

        dgrad_ref[...] += dense_left(gio, ctx_ref[sl, :])
        ugrad_ref[...] += dense_left(io[sl, :], ga)

    @pl.when(step == pl.num_programs(0) - 1)
    def _():
        for t in range(2, len(chunks)):
            mover.sent(t)


def layer(length, adapter, x, cot, gain_one, gain_two, shard_set, n_rep, n_shard, tile, lanes=128, n_rb=4):
    zs, ys = mesh_split(n_rep, n_shard)
    qkv_s, adn_s, aup_s, out_s, up_s, down_s = shard_set
    seq, dim = x.shape
    ff = up_s.shape[1]
    heads = lanes // HEAD
    packed = tile * (seq // tile) * (seq // tile + 1) // 2
    rows = seq // n_rb
    span = ff // zs
    every = tuple(range(zs))
    part = adn_s.shape[1]
    chunks = [(w, every, adn_s.shape[0], 0, part, None) for w in (ADN, AUP)]
    for c in range(0, dim, part):
        chunks += [(QKV, every, qkv_s.shape[0], k * dim + c, part, None) for k in range(3)]
    chunks += [(OUT, every, out_s.shape[0], c, part, None) for c in range(0, dim, part)]
    for k in range(zs):
        chunks += [(DOWN, (k,), down_s.shape[0], c, part, None) for c in range(0, dim, part)]
        chunks += [(UP, every, up_s.shape[0], c, part, (k, span)) for c in range(0, span, part)]
    n = len(chunks)
    plan = Plan(dim // part, part // lanes, zs, n_rb, n, AHEAD)

    def whole(shape):
        return pl.BlockSpec(shape, lambda j: (0, 0), pipeline_mode=pl.Buffered(1))

    def late(j):
        return (jnp.maximum(j - plan.end, 0), 0)

    def pair(j):
        at = jnp.minimum(jnp.maximum(j - plan.att[0], 0), plan.pairs - 1)
        for base in plan.att[1:]:
            at = at + jnp.minimum(jnp.maximum(j - base + 1, 0), plan.pairs)
        return (at, 0, 0)

    row = pl.BlockSpec((rows, dim), late)
    hbm = pl.BlockSpec(memory_space=pl.ANY)
    smem = pl.BlockSpec(memory_space=pltpu.SMEM)
    return pl.pallas_call(
        functools.partial(layer_body, zs, ys, tile, chunks, plan, n_rb),
        grid=(plan.steps,),
        out_shape=[
            jax.ShapeDtypeStruct((zs, ys) + qkv_s.shape, BF),
            jax.ShapeDtypeStruct((seq, 3 * dim), BF),
            jax.ShapeDtypeStruct((seq, COLS), BF),
            jax.ShapeDtypeStruct((dim, COLS), BF),
            jax.ShapeDtypeStruct((dim, COLS), BF),
            jax.ShapeDtypeStruct((seq, dim), BF),
            jax.ShapeDtypeStruct((dim // HEAD, tile, packed), BF),
            jax.ShapeDtypeStruct((seq, dim), BF),
            jax.ShapeDtypeStruct((seq, dim), F32),
            jax.ShapeDtypeStruct((seq, dim), BF),
            jax.ShapeDtypeStruct((COLS, dim), F32),
            jax.ShapeDtypeStruct((COLS, dim), F32),
        ],
        in_specs=[
            smem, smem, whole((seq, dim)),
            pl.BlockSpec((rows, dim), lambda j: (lax.rem(jnp.maximum(j - plan.ff, 0), n_rb), 0)),
            whole((1, dim)), whole((1, dim)), pl.BlockSpec(memory_space=pltpu.VMEM),
            hbm, hbm, hbm, hbm, hbm,
        ],
        out_specs=[
            hbm, whole((seq, 3 * dim)), whole((seq, COLS)), whole((dim, COLS)), whole((dim, COLS)), whole((seq, dim)),
            pl.BlockSpec((heads, tile, packed), pair),
            row, row, row, whole((COLS, dim)), whole((COLS, dim)),
        ],
        scratch_shapes=[
            pltpu.VMEM((zs, ys) + adn_s.shape, BF),
            pltpu.VMEM((zs, ys) + aup_s.shape, BF),
            pltpu.VMEM((zs, ys) + out_s.shape, BF),
            pltpu.VMEM((zs, ys) + up_s.shape, BF),
            pltpu.VMEM((zs, ys) + down_s.shape, BF),
            pltpu.VMEM((seq, dim), F32),
            pltpu.VMEM((seq, dim), F32),
            pltpu.VMEM((seq, dim), F32),
            pltpu.VMEM((seq, dim), BF),
            pltpu.VMEM((seq, COLS), BF),
            pltpu.SemaphoreType.DMA((6,)),
            pltpu.SemaphoreType.DMA,
        ]
        + [pltpu.SemaphoreType.DMA((n,))] * 8,
        compiler_params=pltpu.CompilerParams(collective_id=0, has_side_effects=True, vmem_limit_bytes=66_500_000),
        name="layer_with_gather",
    )(length, adapter, x, cot, gain_one, gain_two, qkv_s, adn_s, aup_s, out_s, up_s, down_s)


def one_slot(tokens, slot_cot, length, adapter, shard_set, gain_one, gain_two, n_rep, n_shard):
    tile = 256 if tokens.shape[0] % 256 == 0 else tokens.shape[0]
    g_one, g_two = gain_one[None], gain_two[None]
    qkv, proj, inner, adn, aup, ctx, probs, y, gh, gc, dg, ug = layer(
        length, adapter, tokens, slot_cot, g_one, g_two, shard_set, n_rep, n_shard, tile
    )
    dq, dk, dv = attention_backward(proj, gc, ctx, probs, tile)
    qkv = qkv.reshape(-1, qkv.shape[-1])
    gx, pay = tail_backward(tokens, gh, inner, dq, dk, dv, g_one, qkv, adn, aup, dg, ug, adapter, n_shard)
    return y, gx, pay


PAY = 2 * COLS + 16


def flip(value, bit):
    return value + bit - 2 * bit * lax.rem(value // bit, 2)


def reduce_body(n_rep, n_shard, bits, pay_ref, down_ref, up_ref, buf, send, recv, xsend, xrecv, lsem):
    r = lax.axis_index("rep")
    s = lax.axis_index("shard")
    others = [lax.rem(s + k, n_shard) for k in range(1, n_shard)]
    peers = [(r, o) for o in others] + [(flip(r, b), s) for b in bits]
    own = pltpu.make_async_copy(pay_ref.at[s], buf.at[r, s], lsem)
    own.start()
    bar = pltpu.get_barrier_semaphore()
    for p in peers:
        pl.semaphore_signal(bar, inc=1, device_id=p, device_id_type=MESH)
    pl.semaphore_wait(bar, len(peers))
    copies = []
    for k, o in enumerate(others):
        cp = pltpu.make_async_remote_copy(
            src_ref=pay_ref.at[o], dst_ref=buf.at[r, s], send_sem=send.at[k], recv_sem=recv.at[k],
            device_id=(r, o), device_id_type=MESH,
        )
        cp.start()
        copies.append(cp)
    own.wait()
    for cp in copies:
        cp.wait()
    held = [0]
    at = 0
    for b in bits:
        partner = flip(r, b)
        copies = []
        for m in held:
            q = r
            for c in bits:
                if m & c:
                    q = flip(q, c)
            cp = pltpu.make_async_remote_copy(
                src_ref=buf.at[q], dst_ref=buf.at[q], send_sem=xsend.at[at], recv_sem=xrecv.at[at],
                device_id=(partner, s), device_id_type=MESH,
            )
            cp.start()
            copies.append(cp)
            at += 1
        for cp in copies:
            cp.wait()
        held = held + [m | b for m in held]
    rows = buf.shape[3]
    for a in range(ADAPTERS):

        def add(i, acc):
            low = buf[i // n_shard, lax.rem(i, n_shard)]
            block = low[: 2 * COLS, :].astype(F32)
            mark = low[2 * COLS : 2 * COLS + 8, :].astype(F32)[0:1, :]
            return acc + jnp.where(mark == float(a), block, 0.0)

        total = lax.fori_loop(0, n_rep * n_shard, add, jnp.zeros((2 * COLS, rows), F32), unroll=4)
        flat = jnp.transpose(total)
        down_ref[:, pl.ds(a * COLS, COLS)] = flat[:, :COLS]
        up_ref[:, pl.ds(a * COLS, COLS)] = flat[:, COLS:]


def reduce_grads(pay, n_rep, n_shard):
    bits = [1 << k for k in range(1, n_rep.bit_length() - 1)] + [1]
    rows = pay.shape[2]
    return pl.pallas_call(
        functools.partial(reduce_body, n_rep, n_shard, bits),
        out_shape=[jax.ShapeDtypeStruct((rows, ADAPTERS * COLS), F32)] * 2,
        in_specs=[pl.BlockSpec(memory_space=pltpu.VMEM)],
        out_specs=[pl.BlockSpec(memory_space=pltpu.VMEM)] * 2,
        scratch_shapes=[pltpu.VMEM((n_rep, n_shard, PAY, rows), BF)]
        + [pltpu.SemaphoreType.DMA((n_shard - 1,))] * 2
        + [pltpu.SemaphoreType.DMA((n_rep - 1,))] * 2
        + [pltpu.SemaphoreType.DMA],
        compiler_params=pltpu.CompilerParams(collective_id=1, has_side_effects=True, vmem_limit_bytes=VMEM_CAP),
        name="reduce_grads",
    )(pay)


def shards(
    inputs,
    cotangent,
    lengths,
    adapter_ids,
    gain_one,
    gain_two,
    qkv_weight,
    out_weight,
    up_weight,
    down_weight,
    adapter_down,
    adapter_up,
):
    n_rep, n_shard = lax.axis_size("rep"), lax.axis_size("shard")
    shard_set = (qkv_weight, adapter_down, adapter_up, out_weight, up_weight, down_weight)
    output, grad, pay = one_slot(
        inputs[0], cotangent[0], lengths, adapter_ids, shard_set, gain_one, gain_two, n_rep, n_shard
    )
    down_grad, up_grad = reduce_grads(pay, n_rep, n_shard)
    return (output[None], grad[None], down_grad, up_grad)


def solution(mesh):
    return jax.shard_map(
        shards,
        mesh=mesh,
        in_specs=(
            P(("rep", "shard"), None, None),
            P(("rep", "shard"), None, None),
            P(("rep", "shard")),
            P(("rep", "shard")),
            P(),
            P(),
            P("shard", None),
            P("shard", None),
            P("shard", None),
            P("shard", None),
            P("shard", None),
            P("shard", None),
        ),
        out_specs=(
            P(("rep", "shard"), None, None),
            P(("rep", "shard"), None, None),
            P("shard", None),
            P("shard", None),
        ),
        check_vma=False,
    )
```

profile of v0, /device:TPU:13, one launch (start us, length us, event | category | flops | bytes accessed | tf_op | source)
XLA Modules:
  0.0 256.8 jit_solution(14574825499064179393)
XLA Ops:
  1.9 176.6 %layer_with_gather.1 = (bf16[4,2,128,3072]{3,2,1,0:T(8,128)(2,1)}, bf16[1024,3072]{1,0:T(8,128)(2,1)}, bf16[1024,64]{1,0:T(8,128)(2,1)}, bf16[1024,64]{1,0:T(8,1...) custom-call(s32[1]{0:T(128)S(6)} %copy.19.len_ref, ...), custom_call_target="tpu_custom_call" | custom-call | tf_op jit(solution)/shard_map/layer_with_gather/pallas_call | solution.py:647
  178.6 32.4 %attention_backward.1 = (bf16[1024,1024]{1,0:T(8,128)(2,1)}, bf16[1024,1024]{1,0:T(8,128)(2,1)}, bf16[1024,1024]{1,0:T(8,128)(2,1)}) custom-call(bf16[1024,3072]{1,0:T(8,128)(2,1)} %get-tuple-element.26.q_ref.k_ref.v_ref, bf16[1024,3072]{1,0:T(8,128)(2,1)} %get-tuple-element.26.q_ref.k_ref.v_ref, bf16[1024,3072]{1,0:T(8,128)(2,1)} %get-tuple-element.26.q_ref.k_ref.v_ref, ...), custom_call_target="tpu_custom_call" | custom-call | tf_op jit(solution)/shard_map/attention_backward/pallas_call | solution.py:125
  211.0 0.0 copy-start
  211.0 18.4 %tail_backward.1 = (bf16[1024,1024]{1,0:T(8,128)(2,1)}, bf16[8,144,128]{2,1,0:T(8,128)(2,1)}) custom-call(bf16[1024,1024]{1,0:T(8,128)(2,1)} %bitcast.8, f32[1024,1024]{1,0:T(8,128)} %get-tuple-element.24.gh_ref, bf16[1024,64]{1,0:T(8,128)(2,1)} %get-tuple-element.25.inner_ref, bf16[1024,1024]{1,0:T(8,128)(2,1)} %get-tuple-element.30.dq_ref, ...), custom_call_target="tpu_custom_call" | custom-call | tf_op jit(solution)/shard_map/tail_backward/pallas_call | solution.py:186
  229.4 24.6 %reduce_grads.1 = (f32[128,512]{1,0:T(8,128)}, f32[128,512]{1,0:T(8,128)}) custom-call(bf16[8,144,128]{2,1,0:T(8,128)(2,1)} %get-tuple-element.39.pay_ref), custom_call_target="tpu_custom_call" | custom-call | tf_op jit(solution)/shard_map/reduce_grads/pallas_call | solution.py:774
  254.0 0.0 copy-done
  254.0 0.0 copy-start.2
  254.0 0.0 copy-start.1
  254.0 1.3 copy.21
  255.4 0.0 copy-done.2
  255.4 0.7 copy.22
  256.1 0.0 copy-done.1
  256.1 0.7 copy.23
Async XLA Ops:
  211.0 43.1 %copy-start = (bf16[1024,1024]{1,0:T(8,128)(2,1)S(1)}, bf16[1024,1024]{1,0:T(8,128)(2,1)}, u32[]{:S(2)}) copy-start(bf16[1024,1024]{1,0:T(8,128)(2,1)} %get-tuple-element.23) | copy-start | bytes 6291460
  254.0 1.3 copy-start.2
  254.0 2.0 copy-start.1
where the time goes:
time: 257 us
  Pallas kernels  252 us (98%)
  local copies, waits for them, and re-layouts  2.74 us (1%)
    pallas_call x1, Pallas kernels, layer(): pl.pallas_call(functools.partial(layer_body, zs, ys, tile, chunks, plan,...  177 us
    pallas_call x1, Pallas kernels, attention_backward(): pl.pallas_call(functools.partial(attn_bwd_body, tile), grid=(n,), out_sha...  32.4 us
    pallas_call x1, Pallas kernels, reduce_grads(): pl.pallas_call(functools.partial(reduce_body, n_rep, n_shard, bits), out_...  24.6 us
    pallas_call x1, Pallas kernels, tail_backward(): pl.pallas_call(tail_body, grid=(seq // rows,), out_shape=[jax.ShapeDtypeS...  18.4 us

commit v1 on v0

--- a/solution.py
+++ b/solution.py
@@ -83,7 +83,10 @@
         off += stop
 
 
-def attn_bwd_body(tile, q_ref, k_ref, v_ref, go_ref, ctx_ref, p_ref, dq_ref, dk_ref, dv_ref, dk_acc, dv_acc):
+def attn_bwd_body(
+    tile, q_ref, k_ref, v_ref, go_ref, ctx_ref, p_ref, y_ref, dq_ref, dk_ref, dv_ref, keep_ref, dk_acc, dv_acc
+):
+    keep_ref[...] = y_ref[...]
     seq, lanes = q_ref.shape
     heads = lanes // HEAD
     scale = HEAD ** (-0.5)
@@ -115,91 +118,25 @@
     dv_ref[...] = dv_acc[...].astype(BF)
 
 
-def attention_backward(proj, grad_ctx, ctx, probs, tile, lanes=128):
+def attention_backward(proj, grad_ctx, ctx, probs, y, tile, lanes=128):
     seq = proj.shape[0]
     width = proj.shape[1] // 3
     n = width // lanes
     heads = lanes // HEAD
     packed = probs.shape[2]
     blk = pl.BlockSpec((seq, lanes), lambda j: (0, j))
+    part = pl.BlockSpec((seq // n, width), lambda j: (j, 0))
     return pl.pallas_call(
         functools.partial(attn_bwd_body, tile),
         grid=(n,),
-        out_shape=[jax.ShapeDtypeStruct((seq, width), BF)] * 3,
+        out_shape=[jax.ShapeDtypeStruct((seq, width), BF)] * 4,
         in_specs=[pl.BlockSpec((seq, lanes), lambda j, t=t: (0, t * n + j)) for t in range(3)]
-        + [blk, blk, pl.BlockSpec((heads, tile, packed), lambda j: (j, 0, 0))],
-        out_specs=[blk] * 3,
+        + [blk, blk, pl.BlockSpec((heads, tile, packed), lambda j: (j, 0, 0)), part],
+        out_specs=[blk, blk, blk, part],
         scratch_shapes=[pltpu.VMEM((seq, lanes), F32)] * 2,
         compiler_params=pltpu.CompilerParams(vmem_limit_bytes=VMEM_CAP),
         name="attention_backward",
-    )(proj, proj, proj, grad_ctx, ctx, probs)
-
-
-def tail_body(
-    x_ref, gh_ref, inner_ref, dq_ref, dk_ref, dv_ref, g_ref, w_ref, adn_ref, aup_ref, din_ref, uin_ref,
-    id_ref, gx_ref, pay_ref, dgrad_ref, ugrad_ref,
-):
-    step = pl.program_id(0)
-    dim = x_ref.shape[1]
-    thirds = [dq_ref[...], dk_ref[...], dv_ref[...]]
-    gi = None
-    gn = None
-    for p in range(3):
-        one = lane_group(dense(thirds[p], aup_ref[...]), RANK, p)
-        gi = one if gi is None else gi + one
-        g = dense_trans(thirds[p], w_ref[:, pl.ds(p * dim, dim)])
-        gn = g if gn is None else gn + g
-    gi = gi.astype(BF)
-    gn = gn + dense_trans(gi, adn_ref[...])
-    unit, rs = norm_stats(x_ref[...].astype(F32))
-    normed = (unit * g_ref[...]).astype(BF)
-    gx_ref[...] = (gh_ref[...] + norm_back(unit, rs, g_ref[...], gn)).astype(BF)
-
-    @pl.when(step == 0)
-    def _():
-        dgrad_ref[...] = din_ref[...]
-        ugrad_ref[...] = uin_ref[...]
-
-    dgrad_ref[...] += dense_left(gi, normed)
-    up = None
-    for p in range(3):
-        one = dense_left(lane_group(inner_ref[...], RANK, p), thirds[p])
-        up = one if up is None else up + one
-    ugrad_ref[...] += up
-
-    @pl.when(step == pl.num_programs(0) - 1)
-    def _():
-        n, pay, width = pay_ref.shape
-        mark = jnp.full((pay - 2 * COLS, width), id_ref[0], jnp.int32).astype(F32)
-        for i in range(n):
-            sl = pl.ds(i * width, width)
-            pay_ref[i] = jnp.concatenate([dgrad_ref[:, sl], ugrad_ref[:, sl], mark], axis=0).astype(BF)
-
-
-def tail_backward(x, gh, inner, dq, dk, dv, gain, qkv, adn, aup, din, uin, adapter, n_shard, rows=256):
-    seq, dim = x.shape
-    row = pl.BlockSpec((rows, dim), lambda i: (i, 0))
-
-    def whole(shape):
-        return pl.BlockSpec(shape, lambda i: (0, 0), pipeline_mode=pl.Buffered(1))
-
-    return pl.pallas_call(
-        tail_body,
-        grid=(seq // rows,),
-        out_shape=[
-            jax.ShapeDtypeStruct((seq, dim), BF),
-            jax.ShapeDtypeStruct((n_shard, PAY, dim // n_shard), BF),
-        ],
-        in_specs=[
-            row, row, pl.BlockSpec((rows, COLS), lambda i: (i, 0)), row, row, row,
-            whole((1, dim)), whole(qkv.shape), whole((dim, COLS)), whole((dim, COLS)), whole((COLS, dim)), whole((COLS, dim)),
-            pl.BlockSpec(memory_space=pltpu.SMEM),
-        ],
-        out_specs=[row, pl.BlockSpec((n_shard, PAY, dim // n_shard), lambda i: (0, 0, 0))],
-        scratch_shapes=[pltpu.VMEM((COLS, dim), F32)] * 2,
-        compiler_params=pltpu.CompilerParams(vmem_limit_bytes=VMEM_CAP),
-        name="tail_backward",
-    )(x, gh, inner, dq, dk, dv, gain, qkv, adn, aup, din, uin, adapter)
+    )(proj, proj, proj, grad_ctx, ctx, probs, y)
 
 
 class Mover:
@@ -698,10 +635,9 @@
     qkv, proj, inner, adn, aup, ctx, probs, y, gh, gc, dg, ug = layer(
         length, adapter, tokens, slot_cot, g_one, g_two, shard_set, n_rep, n_shard, tile
     )
-    dq, dk, dv = attention_backward(proj, gc, ctx, probs, tile)
+    dq, dk, dv, y = attention_backward(proj, gc, ctx, probs, y, tile)
     qkv = qkv.reshape(-1, qkv.shape[-1])
-    gx, pay = tail_backward(tokens, gh, inner, dq, dk, dv, g_one, qkv, adn, aup, dg, ug, adapter, n_shard)
-    return y, gx, pay
+    return y, *tail_backward(tokens, gh, inner, dq, dk, dv, g_one, qkv, adn, aup, dg, ug, adapter, n_rep, n_shard)
 
 
 PAY = 2 * COLS + 16
@@ -711,78 +647,166 @@
     return value + bit - 2 * bit * lax.rem(value // bit, 2)
 
 
-def reduce_body(n_rep, n_shard, bits, pay_ref, down_ref, up_ref, buf, send, recv, xsend, xrecv, lsem):
+def tail_body(
+    n_rep, n_shard, bits, nb, x_ref, gh_ref, inner_ref, dq_ref, dk_ref, dv_ref, g_ref, w_ref, adn_ref, aup_ref,
+    din_ref, uin_ref, id_ref, gx_ref, down_ref, up_ref, gi_s, dgrad, ugrad, pay, buf, send, recv, xsend, xrecv, lsem,
+):
+    step = pl.program_id(0)
+    rows, dim = x_ref.shape
     r = lax.axis_index("rep")
     s = lax.axis_index("shard")
     others = [lax.rem(s + k, n_shard) for k in range(1, n_shard)]
     peers = [(r, o) for o in others] + [(flip(r, b), s) for b in bits]
-    own = pltpu.make_async_copy(pay_ref.at[s], buf.at[r, s], lsem)
-    own.start()
-    bar = pltpu.get_barrier_semaphore()
-    for p in peers:
-        pl.semaphore_signal(bar, inc=1, device_id=p, device_id_type=MESH)
-    pl.semaphore_wait(bar, len(peers))
-    copies = []
-    for k, o in enumerate(others):
-        cp = pltpu.make_async_remote_copy(
-            src_ref=pay_ref.at[o], dst_ref=buf.at[r, s], send_sem=send.at[k], recv_sem=recv.at[k],
+    own = pltpu.make_async_copy(pay.at[s], buf.at[r, s], lsem)
+    first = [
+        pltpu.make_async_remote_copy(
+            src_ref=pay.at[o], dst_ref=buf.at[r, s], send_sem=send.at[k], recv_sem=recv.at[k],
             device_id=(r, o), device_id_type=MESH,
         )
-        cp.start()
-        copies.append(cp)
-    own.wait()
-    for cp in copies:
-        cp.wait()
-    held = [0]
-    at = 0
+        for k, o in enumerate(others)
+    ]
+    rounds = []
+    held, at = [0], 0
     for b in bits:
-        partner = flip(r, b)
         copies = []
         for m in held:
             q = r
             for c in bits:
                 if m & c:
                     q = flip(q, c)
-            cp = pltpu.make_async_remote_copy(
-                src_ref=buf.at[q], dst_ref=buf.at[q], send_sem=xsend.at[at], recv_sem=xrecv.at[at],
-                device_id=(partner, s), device_id_type=MESH,
+            copies.append(
+                pltpu.make_async_remote_copy(
+                    src_ref=buf.at[q], dst_ref=buf.at[q], send_sem=xsend.at[at], recv_sem=xrecv.at[at],
+                    device_id=(flip(r, b), s), device_id_type=MESH,
+                )
             )
+            at += 1
+        rounds.append(copies)
+        held = held + [m | b for m in held]
+
+    def block_sl():
+        return pl.ds(pl.multiple_of(lax.rem(step, nb) * rows, rows), rows)
+
+    @pl.when(step == 0)
+    def _():
+        dgrad[...] = din_ref[...]
+        ugrad[...] = uin_ref[...]
+
+    @pl.when(step < nb)
+    def _():
+        thirds = [dq_ref[...], dk_ref[...], dv_ref[...]]
+        gi, up = None, None
+        for p in range(3):
+            one = lane_group(dense(thirds[p], aup_ref[...]), RANK, p)
+            gi = one if gi is None else gi + one
+            two = dense_left(lane_group(inner_ref[...], RANK, p), thirds[p])
+            up = two if up is None else up + two
+        gi = gi.astype(BF)
+        gi_s[block_sl(), :] = gi
+        unit, _ = norm_stats(x_ref[...].astype(F32))
+        dgrad[...] += dense_left(gi, (unit * g_ref[...]).astype(BF))
+        ugrad[...] += up
+
+    @pl.when(step == nb - 1)
+    def _():
+        width = pay.shape[2]
+        mark = jnp.full((PAY - 2 * COLS, width), id_ref[0], jnp.int32).astype(F32)
+        for i in range(n_shard):
+            sl = pl.ds(i * width, width)
+            pay[i] = jnp.concatenate([dgrad[:, sl], ugrad[:, sl], mark], axis=0).astype(BF)
+        bar = pltpu.get_barrier_semaphore()
+        for p in peers:
+            pl.semaphore_signal(bar, inc=1, device_id=p, device_id_type=MESH)
+        pl.semaphore_wait(bar, len(peers))
+
+    @pl.when(step == nb)
+    def _():
+        own.start()
+        for cp in first:
             cp.start()
-            copies.append(cp)
-            at += 1
-        for cp in copies:
+
+    @pl.when(step == nb + nb // 2)
+    def _():
+        own.wait()
+        for cp in first:
             cp.wait()
-        held = held + [m | b for m in held]
-    rows = buf.shape[3]
-    for a in range(ADAPTERS):
-
-        def add(i, acc):
-            low = buf[i // n_shard, lax.rem(i, n_shard)]
-            block = low[: 2 * COLS, :].astype(F32)
-            mark = low[2 * COLS : 2 * COLS + 8, :].astype(F32)[0:1, :]
-            return acc + jnp.where(mark == float(a), block, 0.0)
-
-        total = lax.fori_loop(0, n_rep * n_shard, add, jnp.zeros((2 * COLS, rows), F32), unroll=4)
-        flat = jnp.transpose(total)
-        down_ref[:, pl.ds(a * COLS, COLS)] = flat[:, :COLS]
-        up_ref[:, pl.ds(a * COLS, COLS)] = flat[:, COLS:]
-
-
-def reduce_grads(pay, n_rep, n_shard):
+        for cp in rounds[0]:
+            cp.start()
+
+    @pl.when((step >= nb) & (step < 2 * nb))
+    def _():
+        thirds = [dq_ref[...], dk_ref[...], dv_ref[...]]
+        gn = dense_trans(gi_s[block_sl(), :], adn_ref[...])
+        for p in range(3):
+            gn = gn + dense_trans(thirds[p], w_ref[:, pl.ds(p * dim, dim)])
+        unit, rs = norm_stats(x_ref[...].astype(F32))
+        gx_ref[...] = (gh_ref[...] + norm_back(unit, rs, g_ref[...], gn)).astype(BF)
+
+    @pl.when(step == 2 * nb)
+    def _():
+        for cp in rounds[0]:
+            cp.wait()
+        for copies in rounds[1:]:
+            for cp in copies:
+                cp.start()
+            for cp in copies:
+                cp.wait()
+        width = buf.shape[3]
+        for a in range(ADAPTERS):
+
+            def add(i, acc):
+                low = buf[i // n_shard, lax.rem(i, n_shard)]
+                block = low[: 2 * COLS, :].astype(F32)
+                mark = low[2 * COLS : 2 * COLS + 8, :].astype(F32)[0:1, :]
+                return acc + jnp.where(mark == float(a), block, 0.0)
+
+            total = lax.fori_loop(0, n_rep * n_shard, add, jnp.zeros((2 * COLS, width), F32), unroll=4)
+            flat = jnp.transpose(total)
+            down_ref[:, pl.ds(a * COLS, COLS)] = flat[:, :COLS]
+            up_ref[:, pl.ds(a * COLS, COLS)] = flat[:, COLS:]
+
+
+def tail_backward(x, gh, inner, dq, dk, dv, gain, qkv, adn, aup, din, uin, adapter, n_rep, n_shard, rows=256):
+    seq, dim = x.shape
+    nb = seq // rows
     bits = [1 << k for k in range(1, n_rep.bit_length() - 1)] + [1]
-    rows = pay.shape[2]
+    width = dim // n_shard
+
+    def both(j):
+        return (lax.rem(jnp.minimum(j, 2 * nb - 1), nb), 0)
+
+    def second(j):
+        return (jnp.minimum(jnp.maximum(j - nb, 0), nb - 1), 0)
+
+    def whole(shape):
+        return pl.BlockSpec(shape, lambda j: (0, 0), pipeline_mode=pl.Buffered(1))
+
+    row = pl.BlockSpec((rows, dim), both)
+    late = pl.BlockSpec((rows, dim), second)
     return pl.pallas_call(
-        functools.partial(reduce_body, n_rep, n_shard, bits),
-        out_shape=[jax.ShapeDtypeStruct((rows, ADAPTERS * COLS), F32)] * 2,
-        in_specs=[pl.BlockSpec(memory_space=pltpu.VMEM)],
-        out_specs=[pl.BlockSpec(memory_space=pltpu.VMEM)] * 2,
-        scratch_shapes=[pltpu.VMEM((n_rep, n_shard, PAY, rows), BF)]
+        functools.partial(tail_body, n_rep, n_shard, bits, nb),
+        grid=(2 * nb + 1,),
+        out_shape=[jax.ShapeDtypeStruct((seq, dim), BF)]
+        + [jax.ShapeDtypeStruct((width, ADAPTERS * COLS), F32)] * 2,
+        in_specs=[
+            row, late, pl.BlockSpec((rows, COLS), both), row, row, row,
+            whole((1, dim)), whole(qkv.shape), whole((dim, COLS)), whole((dim, COLS)), whole((COLS, dim)), whole((COLS, dim)),
+            pl.BlockSpec(memory_space=pltpu.SMEM),
+        ],
+        out_specs=[late, whole((width, ADAPTERS * COLS)), whole((width, ADAPTERS * COLS))],
+        scratch_shapes=[
+            pltpu.VMEM((seq, COLS), BF),
+            pltpu.VMEM((COLS, dim), F32),
+            pltpu.VMEM((COLS, dim), F32),
+            pltpu.VMEM((n_shard, PAY, width), BF),
+            pltpu.VMEM((n_rep, n_shard, PAY, width), BF),
+        ]
         + [pltpu.SemaphoreType.DMA((n_shard - 1,))] * 2
         + [pltpu.SemaphoreType.DMA((n_rep - 1,))] * 2
         + [pltpu.SemaphoreType.DMA],
         compiler_params=pltpu.CompilerParams(collective_id=1, has_side_effects=True, vmem_limit_bytes=VMEM_CAP),
-        name="reduce_grads",
-    )(pay)
+        name="tail_and_reduce",
+    )(x, gh, inner, dq, dk, dv, gain, qkv, adn, aup, din, uin, adapter)
 
 
 def shards(
@@ -801,10 +825,9 @@
 ):
     n_rep, n_shard = lax.axis_size("rep"), lax.axis_size("shard")
     shard_set = (qkv_weight, adapter_down, adapter_up, out_weight, up_weight, down_weight)
-    output, grad, pay = one_slot(
+    output, grad, down_grad, up_grad = one_slot(
         inputs[0], cotangent[0], lengths, adapter_ids, shard_set, gain_one, gain_two, n_rep, n_shard
     )
-    down_grad, up_grad = reduce_grads(pay, n_rep, n_shard)
     return (output[None], grad[None], down_grad, up_grad)
 
 

time: 257 us -> 250 us (0.973)
  Pallas kernels: 252 us -> 243 us
    pallas_call x2 -> x1, Pallas kernels: 43 us -> 33.4 us  [tail_backward(): pl.pallas_call(functools.partial(tail_body, n_rep, n_shard, bits, nb), gr...]
where the time goes in v1:
time: 250 us; the launch traced here: 249 us
  Pallas kernels  243 us (97%)
  local copies, waits for them, and re-layouts  4.55 us (2%)
    pallas_call x1, Pallas kernels, layer(): pl.pallas_call(functools.partial(layer_body, zs, ys, tile, chunks, plan,...  177 us
    pallas_call x1, Pallas kernels, tail_backward(): pl.pallas_call(functools.partial(tail_body, n_rep, n_shard, bits, nb), gr...  33.4 us
    pallas_call x1, Pallas kernels, attention_backward(): pl.pallas_call(functools.partial(attn_bwd_body, tile), grid=(n,), out_sha...  32.5 us

profile of v1, /device:TPU:13, one launch (start us, length us, event | category | flops | bytes accessed | tf_op | source)
XLA Modules:
  0.0 249.1 jit_solution(2383132552331340123)
XLA Ops:
  1.9 176.7 %layer_with_gather.1 = (bf16[4,2,128,3072]{3,2,1,0:T(8,128)(2,1)}, bf16[1024,3072]{1,0:T(8,128)(2,1)}, bf16[1024,64]{1,0:T(8,128)(2,1)}, bf16[1024,64]{1,0:T(8,1...) custom-call(s32[1]{0:T(128)S(6)} %copy.19.len_ref, ...), custom_call_target="tpu_custom_call" | custom-call | tf_op jit(solution)/shard_map/layer_with_gather/pallas_call | solution.py:584
  178.7 32.5 %attention_backward.1 = (bf16[1024,1024]{1,0:T(8,128)(2,1)}, bf16[1024,1024]{1,0:T(8,128)(2,1)}, bf16[1024,1024]{1,0:T(8,128)(2,1)}, bf16[1024,1024]{1,0:T(8,128)(2,1)}) custom-call(bf16[1024,3072]{1,0:T(8,128)(2,1)} %get-tuple-element.23.q_ref.k_ref.v_ref, bf16[1024,3072]{1,0:T(8,128)(2,1)} %get-tuple-element.23.q_ref.k_ref.v_ref, ...), custom_call_target="tpu_custom_call" | custom-call | tf_op jit(solution)/shard_map/attention_backward/pallas_call | solution.py:129
  211.1 33.4 %tail_and_reduce.1 = (bf16[1024,1024]{1,0:T(8,128)(2,1)}, f32[128,512]{1,0:T(8,128)}, f32[128,512]{1,0:T(8,128)}) custom-call(bf16[1024,1024]{1,0:T(8,128)(2,1)} %bitcast.8, f32[1024,1024]{1,0:T(8,128)} %get-tuple-element.29.gh_ref, bf16[1024,64]{1,0:T(8,128)(2,1)} %get-tuple-element.30.inner_ref, bf16[1024,1024]{1,0:T(8,128)(2,1)} %get-tuple-element.31.dq_ref, ...), custom_call_target="tpu_custom_call" | custom-call | tf_op jit(solution)/shard_map/tail_and_reduce/pallas_call | solution.py:786
  244.5 0.0 copy-start.1
  244.5 0.0 copy-start
  244.5 3.1 %copy.21 = bf16[1,1024,1024]{2,1,0:T(8,128)(2,1)} copy(bf16[1,1024,1024]{2,1,0:T(8,128)(2,1)} %bitcast.11) | data formatting | bytes 4194304
  247.6 0.0 copy-done.1
  247.6 0.7 copy.22
  248.4 0.0 copy-done
  248.4 0.7 copy.23
Async XLA Ops:
  244.5 3.2 %copy-start.1 = (f32[128,512]{1,0:T(8,128)S(1)}, f32[128,512]{1,0:T(8,128)}, u32[]{:S(2)}) copy-start(f32[128,512]{1,0:T(8,128)} %get-tuple-element.48) | copy-start | bytes 786436
  244.5 3.9 %copy-start = (f32[128,512]{1,0:T(8,128)S(1)}, f32[128,512]{1,0:T(8,128)}, u32[]{:S(2)}) copy-start(f32[128,512]{1,0:T(8,128)} %get-tuple-element.49) | copy-start | bytes 786436

commit v2 on v1

--- a/solution.py
+++ b/solution.py
@@ -219,14 +219,14 @@
                 self.send(self.shards[w].at[mine, col], w, self.z, self.y, mine, col, t, 1, (self.r, self.z * self.ys + v))
 
     def begin(self):
-        for t in range(min(self.ahead, len(self.chunks))):
+        for t in self.ahead[-1]:
             self.start_z(t)
             self.start_y(t)
 
     def relay_z(self, m):
-        if m + self.ahead < len(self.chunks):
-            self.start_z(m + self.ahead)
-            self.start_y(m + self.ahead)
+        for t in self.ahead[m]:
+            self.start_z(t)
+            self.start_y(t)
         w, offs, rows, a, half, mine, excl, missing, col = self.geom(m, self.z)
         self.wait(m, 0, 1)
         for o in offs:
@@ -241,10 +241,10 @@
     def relay_y(self, m):
         w, offs, rows, a, half, mine, excl, missing, col = self.geom(m, self.z)
         self.wait(m, 1, 1)
-        for o in offs:
+        for zz in [self.at_z(o) for o in offs]:
             for v in self.ypeers:
-                self.relay(w, self.at_z(o), v, excl, col, m, 2, self.par)
-                self.relay(w, self.at_z(o), v, mine, col, m, 3, self.sib)
+                self.relay(w, zz, v, excl, col, m, 2, self.par)
+                self.relay(w, zz, v, mine, col, m, 3, self.sib)
 
     def relay_x(self, m):
         w, offs, rows, a, half, mine, excl, missing, col = self.geom(m, self.z)
@@ -252,8 +252,9 @@
         for o in offs:
             if o:
                 self.relay(w, self.at_z(o), self.y, missing, col, m, 3, self.sib)
+        for zz in [self.at_z(o) for o in offs]:
             for v in self.ypeers:
-                self.relay(w, self.at_z(o), v, missing, col, m, 3, self.sib)
+                self.relay(w, zz, v, missing, col, m, 3, self.sib)
 
     def tick(self, todo):
         for stage, m in todo:
@@ -269,12 +270,27 @@
 
 QKV, ADN, AUP, OUT, UP, DOWN = range(6)
 AHEAD = 6
+WIDE = 1024
 UNIT = (4.1, 3.9, 4.0)
 
 
+def starts(sizes):
+    out, nxt, open_now = {}, 0, 0
+    for m in range(-1, len(sizes)):
+        open_now -= sizes[m] if m >= 0 else 0
+        out[m] = []
+        while nxt < len(sizes) and open_now + sizes[nxt] <= AHEAD:
+            open_now += sizes[nxt]
+            out[m].append(nxt)
+            nxt += 1
+    return out
+
+
 class Plan:
-    def __init__(self, groups, pairs, zs, n_rb, n, ahead):
+    def __init__(self, groups, pairs, zs, n_rb, sizes, outs):
         self.pairs = pairs
+        n = len(sizes)
+        self.ahead = starts(sizes)
         self.proj, self.att = [], []
         cost = [5.0, 3.0]
         need = {1: [0, 1]}
@@ -287,9 +303,9 @@
             cost += [3.45] * pairs
         done = 2 + 3 * groups
         self.out = len(cost)
-        need[self.out] = list(range(done, done + groups))
+        need[self.out] = list(range(done, done + outs))
         cost.append(6.0)
-        done += groups
+        done += outs
         self.ff = len(cost)
         per = (n - done) // zs
         for f in range(zs):
@@ -299,9 +315,9 @@
         cost += [3.6] * n_rb
         self.steps = len(cost)
         self.ticks = {}
-        self.spread(cost, need, n, ahead)
-
-    def spread(self, cost, need, n, ahead):
+        self.spread(cost, need, n, sizes)
+
+    def spread(self, cost, need, n, sizes):
         hop, now = 1.5, 2.0
         free = [now, now, now]
         due = [{}, {}, {}]
@@ -309,21 +325,21 @@
         ready = {}
 
         def begin(c, t):
-            free[0] = max(free[0], t) + UNIT[0]
+            free[0] = max(free[0], t) + UNIT[0] * sizes[c]
             due[0][c] = free[0] + hop
-            free[1] = max(free[1], t) + UNIT[1] / 4
+            free[1] = max(free[1], t) + UNIT[1] * sizes[c] / 4
 
         def run(stage, t):
             c = nxt[stage]
             nxt[stage] += 1
             if stage == 0:
-                if c + ahead < n:
-                    begin(c + ahead, t)
-                free[1] = max(free[1], t) + UNIT[1] * 0.75
+                for k in self.ahead[c]:
+                    begin(k, t)
+                free[1] = max(free[1], t) + UNIT[1] * 0.75 * sizes[c]
                 due[1][c] = free[1] + hop
-                free[2] = max(free[2], t) + UNIT[2] * 0.43
+                free[2] = max(free[2], t) + UNIT[2] * 0.43 * sizes[c]
             elif stage == 1:
-                free[2] = max(free[2], t) + UNIT[2] * 0.57
+                free[2] = max(free[2], t) + UNIT[2] * 0.57 * sizes[c]
                 due[2][c] = free[2] + hop
             else:
                 ready[c] = t + 2.0
@@ -332,7 +348,7 @@
         def open_ops():
             return [(due[k][nxt[k]], k) for k in range(3) if nxt[k] in due[k]]
 
-        for c in range(min(n, ahead)):
+        for c in self.ahead[-1]:
             begin(c, now)
         for step, spent in enumerate(cost):
             todo = []
@@ -366,7 +382,7 @@
     seq, dim = x_ref.shape
     rows = seq // n_rb
     span = up_v.shape[3] // zs
-    mover = Mover(zs, ys, (qkv_s, adn_s, aup_s, out_s, up_s, down_s), (qkv_f, qa, qb, out_v, up_v, down_v), sems, chunks, AHEAD)
+    mover = Mover(zs, ys, (qkv_s, adn_s, aup_s, out_s, up_s, down_s), (qkv_f, qa, qb, out_v, up_v, down_v), sems, chunks, plan.ahead)
     own = [
         pltpu.make_async_copy(src, land.at[mover.z, mover.y], local.at[i])
         for i, (src, land) in enumerate(zip(mover.shards, mover.lands))
@@ -559,12 +575,14 @@
     chunks = [(w, every, adn_s.shape[0], 0, part, None) for w in (ADN, AUP)]
     for c in range(0, dim, part):
         chunks += [(QKV, every, qkv_s.shape[0], k * dim + c, part, None) for k in range(3)]
-    chunks += [(OUT, every, out_s.shape[0], c, part, None) for c in range(0, dim, part)]
+    wide = min(WIDE, dim, span)
+    chunks += [(OUT, every, out_s.shape[0], c, wide, None) for c in range(0, dim, wide)]
     for k in range(zs):
-        chunks += [(DOWN, (k,), down_s.shape[0], c, part, None) for c in range(0, dim, part)]
-        chunks += [(UP, every, up_s.shape[0], c, part, (k, span)) for c in range(0, span, part)]
+        chunks += [(DOWN, (k,), down_s.shape[0], c, wide, None) for c in range(0, dim, wide)]
+        chunks += [(UP, every, up_s.shape[0], c, wide, (k, span)) for c in range(0, span, wide)]
     n = len(chunks)
-    plan = Plan(dim // part, part // lanes, zs, n_rb, n, AHEAD)
+    sizes = [c[4] // part for c in chunks]
+    plan = Plan(dim // part, part // lanes, zs, n_rb, sizes, dim // wide)
 
     def whole(shape):
         return pl.BlockSpec(shape, lambda j: (0, 0), pipeline_mode=pl.Buffered(1))

time: 250 us -> 250 us (level)
  no operation moved by 1% of the time
where the time goes in v2:
time: 250 us; the launch traced here: 249 us
  Pallas kernels  243 us (97%)
  local copies, waits for them, and re-layouts  4.55 us (2%)
    pallas_call x1, Pallas kernels, layer(): pl.pallas_call(functools.partial(layer_body, zs, ys, tile, chunks, plan,...  176 us
    pallas_call x1, Pallas kernels, tail_backward(): pl.pallas_call(functools.partial(tail_body, n_rep, n_shard, bits, nb), gr...  34.5 us
    pallas_call x1, Pallas kernels, attention_backward(): pl.pallas_call(functools.partial(attn_bwd_body, tile), grid=(n,), out_sha...  32.5 us

profile of v2, /device:TPU:13, one launch (start us, length us, event | category | flops | bytes accessed | tf_op | source)
XLA Modules:
  0.0 249.1 jit_solution(16385452098172688934)
XLA Ops:
  1.9 175.7 %layer_with_gather.1 = (bf16[4,2,128,3072]{3,2,1,0:T(8,128)(2,1)}, bf16[1024,3072]{1,0:T(8,128)(2,1)}, bf16[1024,64]{1,0:T(8,128)(2,1)}, bf16[1024,64]{1,0:T(8,1...) custom-call(s32[1]{0:T(128)S(6)} %copy.19.len_ref, ...), custom_call_target="tpu_custom_call" | custom-call | tf_op jit(solution)/shard_map/layer_with_gather/pallas_call | solution.py:602
  177.6 32.5 %attention_backward.1 = (bf16[1024,1024]{1,0:T(8,128)(2,1)}, bf16[1024,1024]{1,0:T(8,128)(2,1)}, bf16[1024,1024]{1,0:T(8,128)(2,1)}, bf16[1024,1024]{1,0:T(8,128)(2,1)}) custom-call(bf16[1024,3072]{1,0:T(8,128)(2,1)} %get-tuple-element.23.q_ref.k_ref.v_ref, bf16[1024,3072]{1,0:T(8,128)(2,1)} %get-tuple-element.23.q_ref.k_ref.v_ref, ...), custom_call_target="tpu_custom_call" | custom-call | tf_op jit(solution)/shard_map/attention_backward/pallas_call | solution.py:129
  210.1 34.5 %tail_and_reduce.1 = (bf16[1024,1024]{1,0:T(8,128)(2,1)}, f32[128,512]{1,0:T(8,128)}, f32[128,512]{1,0:T(8,128)}) custom-call(bf16[1024,1024]{1,0:T(8,128)(2,1)} %bitcast.8, f32[1024,1024]{1,0:T(8,128)} %get-tuple-element.29.gh_ref, bf16[1024,64]{1,0:T(8,128)(2,1)} %get-tuple-element.30.inner_ref, bf16[1024,1024]{1,0:T(8,128)(2,1)} %get-tuple-element.31.dq_ref, ...), custom_call_target="tpu_custom_call" | custom-call | tf_op jit(solution)/shard_map/tail_and_reduce/pallas_call | solution.py:804
  244.6 0.0 copy-start.1
  244.6 0.0 copy-start
  244.6 3.1 %copy.21 = bf16[1,1024,1024]{2,1,0:T(8,128)(2,1)} copy(bf16[1,1024,1024]{2,1,0:T(8,128)(2,1)} %bitcast.11) | data formatting | bytes 4194304
  247.7 0.0 copy-done.1
  247.7 0.7 copy.22
  248.4 0.0 copy-done
  248.4 0.7 copy.23
Async XLA Ops:
  244.6 3.2 %copy-start.1 = (f32[128,512]{1,0:T(8,128)S(1)}, f32[128,512]{1,0:T(8,128)}, u32[]{:S(2)}) copy-start(f32[128,512]{1,0:T(8,128)} %get-tuple-element.48) | copy-start | bytes 786436
  244.6 3.9 %copy-start = (f32[128,512]{1,0:T(8,128)S(1)}, f32[128,512]{1,0:T(8,128)}, u32[]{:S(2)}) copy-start(f32[128,512]{1,0:T(8,128)} %get-tuple-element.49) | copy-start | bytes 786436
